TPU v7x, 256 devices: a whole 4x4x8 slice. The times are simulated.
256 devices in a mesh: row: 8 (over y_hi, x), col: 32 (over z, y_lo, core).
Axes of the slice: x: 4, y: 4 (y_hi: 2, y_lo: 2; y = y_hi * 2 + y_lo), z: 8, core: 2. Of those that a mesh axis runs over, the one named last changes fastest.
Arguments:
- gradient: bfloat16 [2304, 18432], P('row', 'col'), may hold values from -6 to 6
- left_basis: bfloat16 [2304, 2304], P('row'), may hold values from -0.125 to 0.125
- right_basis: bfloat16 [18432, 18432], P('col', 'row'), may hold values from -0.046875 to 0.046875
- first_moment: float32 [2304, 18432], P('col', 'row'), may hold values from -3 to 3
- second_moment: float32 [2304, 18432], P('col', 'row'), may hold values from 0.25 to 4
Outputs:
- update: bfloat16 [2304, 18432], P('row', 'col')
- first_new: float32 [2304, 18432], P('col', 'row')
- second_new: float32 [2304, 18432], P('col', 'row')
All inputs are finite; a program needn't handle non-finite values.
Results may differ from a plain program's by a relative error of at most 0.018.
Values may be sent and summed in bfloat16 or wider, within the bound.
No kernel may reach another device: no remote copies, remote signals or barrier semaphores. Data moves between devices by JAX's collectives and lax.ppermute only.
A program may use at most 64 MiB of HBM per device.

v0:
```python
import jax
import jax.numpy as jnp
from jax import lax
from jax.sharding import PartitionSpec as P

beta_one = 0.9
beta_two = 0.95
epsilon = 1e-08
correct_one = 1.0 - 0.9**10
correct_two = 1.0 - 0.95**10


def cut_along(shard, dim, size):
    before, after = (shard.shape[:dim], shard.shape[dim + 1 :])
    return jnp.moveaxis(shard.reshape(*before, size, -1, *after), dim, 0)


def sum_at_owner(shard, axis, dim):
    size = lax.axis_size(axis)
    blocks = lax.all_to_all(cut_along(shard, dim, size), axis, 0, 0, tiled=True)
    return jnp.sum(blocks.astype(jnp.float32), axis=0)


def copy_for_each(shard, axis):
    copies = jnp.broadcast_to(shard, (lax.axis_size(axis), *shard.shape))
    return lax.all_to_all(copies, axis, split_axis=0, concat_axis=0, tiled=True)


def in_order(blocks, dim):
    blocks = jnp.moveaxis(blocks, 0, dim)
    dims = blocks.shape
    return blocks.reshape(*dims[:dim], dims[dim] * dims[dim + 1], *dims[dim + 2 :])


def gathered_copies(shard, axis, dim):
    blocks = copy_for_each(shard, axis)
    return in_order(blocks, dim)


def per_device(gradient, left_basis, right_basis, first_moment, second_moment):
    partial_value = lax.dot_general(
        left_basis, gradient, (((0,), (0,)), ((), ())), preferred_element_type=jnp.float32
    )
    rotated_left = lax.psum(partial_value.astype(jnp.bfloat16), "row")
    rotated = lax.psum_scatter(
        jnp.dot(rotated_left, right_basis, preferred_element_type=jnp.float32).astype(jnp.bfloat16),
        "col",
        scatter_dimension=0,
        tiled=True,
    )
    rotated_wide = rotated.astype(jnp.float32)
    first_new = beta_one * first_moment + (1.0 - beta_one) * rotated_wide
    second_new = beta_two * second_moment + (1.0 - beta_two) * rotated_wide * rotated_wide
    step_rot = (first_new / correct_one / (jnp.sqrt(second_new / correct_two) + epsilon)).astype(
        jnp.bfloat16
    )
    back_part = lax.dot_general(
        lax.all_gather(step_rot, "col", axis=0, tiled=True),
        right_basis,
        (((1,), (1,)), ((), ())),
        preferred_element_type=jnp.float32,
    )
    back_own = sum_at_owner(back_part.astype(jnp.bfloat16), "row", 0).astype(jnp.bfloat16)
    back_rot = gathered_copies(back_own, "row", 0)
    update = jnp.dot(left_basis, back_rot, preferred_element_type=jnp.float32).astype(jnp.bfloat16)
    return (update, first_new, second_new)


def solution(mesh):
    in_specs = (P("row", "col"), P("row", None), P("col", "row"), P("col", "row"), P("col", "row"))
    out_specs = (P("row", "col"), P("col", "row"), P("col", "row"))
    return jax.shard_map(
        per_device, mesh=mesh, in_specs=in_specs, out_specs=out_specs, check_vma=False
    )
```

profile of v0, /device:TPU:32, one launch (start us, length us, event | category | flops | bytes accessed | tf_op | source)
XLA Modules:
  0.0 455.3 jit_solution(5712850803293261897)
XLA Ops:
  7.2 0.0 copy-start
  7.2 0.0 all-reduce.2.cloned.1.call-start
  7.2 5.1 %convolution_convert_fusion.1 = bf16[2304,576]{1,0:T(8,128)(2,1)} fusion(bf16[288,2304]{1,0:T(8,128)(2,1)} %param.6, bf16[288,576]{1,0:T(8,128)(2,1)} %param.5), kind=kOutput, calls=%fused_computation.1 | convolution fusion | flops 765739008 | bytes 4313088 | tf_op jit(solution)/shard_map/dot_general | solution.py:41
  12.3 0.0 all-reduce.2.cloned.1.call-update
  12.3 0.0 reduce-scatter.2.cloned.1.call-start
  12.4 106.2 %all-reduce.2.cloned.1.call-done = bf16[2304,576]{1,0:T(8,128)(2,1)} async-done(((bf16[2304,576]{1,0:T(8,128)(2,1)}), bf16[2304,576]{1,0:T(8,128)(2,1)}) %all-reduce.2.cloned.1.call-update) | async-done | bytes 2654224 | tf_op jit(solution)/shard_map/psum | solution.py:44
  118.6 0.0 copy-done
  118.6 12.5 %convolution_convert_fusion = bf16[2304,2304]{1,0:T(8,128)(2,1)} fusion(bf16[2304,576]{1,0:T(8,128)(2,1)} %all-reduce.2.cloned.1.call-done, bf16[576,2304]{1,0:T(8,128)(2,1)S(1)} %copy-done), kind=kOutput, calls=%fused_computation | convolution fusion | flops 6120603648 | bytes 15925248 | tf_op jit(solution)/shard_map/dot_general | solution.py:46
  131.0 0.0 copy-start.1
  131.1 0.0 reduce-scatter.2.cloned.1.call-update
  131.1 0.0 all-gather.2.cloned.1.call-start
  131.1 129.7 %reduce-scatter.2.cloned.1.call-done = bf16[72,2304]{1,0:T(8,128)(2,1)} async-done(((bf16[2304,2304]{1,0:T(8,128)(2,1)}), bf16[72,2304]{1,0:T(8,128)(2,1)}) %reduce-scatter.2.cloned.1.call-update) | async-done | bytes 331792 | tf_op jit(solution)/shard_map/reduce_scatter | solution.py:45
  260.9 0.0 copy-done.1
  260.9 2.6 divide_convert_fusion
  263.4 0.0 all-gather.2.cloned.1.call-update
  263.5 79.1 %all-gather.2.cloned.1.call-done = bf16[2304,2304]{1,0:T(8,128)(2,1)} async-done(((bf16[72,2304]{1,0:T(8,128)(2,1)}), bf16[2304,2304]{1,0:T(8,128)(2,1)}) %all-gather.2.cloned.1.call-update) | async-done | bytes 10616848 | tf_op jit(solution)/shard_map/all_gather | solution.py:58
  342.5 11.7 %convolution_convert_fusion.2 = bf16[2304,576]{0,1:T(8,128)(2,1)} fusion(bf16[2304,2304]{1,0:T(8,128)(2,1)} %all-gather.2.cloned.1.call-done, bf16[576,2304]{1,0:T(8,128)(2,1)S(1)} %copy-done), kind=kOutput, calls=%fused_computation.2 | convolution fusion | flops 6116622336 | bytes 15925248 | tf_op jit(solution)/shard_map/dot_general | solution.py:57
  354.3 4.5 copy.8
  358.8 44.9 %all_to_all.10 = bf16[8,288,576]{2,1,0:T(8,128)(2,1)} all-to-all(bf16[8,288,576]{2,1,0:T(8,128)(2,1)} %bitcast.12), channel_id=1, replica_groups=mesh['row'=8,'col'=32] {'row'}, dimensions={0} | all-to-all | bytes 5308416 | tf_op jit(solution)/shard_map/all_to_all | solution.py:20
  403.7 2.4 reduce_sum.12
  406.1 0.2 broadcast_in_dim.3
  406.3 0.0 copy-start.2
  406.3 40.5 %all_to_all.11 = bf16[8,288,576]{2,1,0:T(8,128)(2,1)S(1)} all-to-all(bf16[8,288,576]{2,1,0:T(8,128)(2,1)S(1)} %broadcast_in_dim.3), channel_id=1, replica_groups=mesh['row'=8,'col'=32] {'row'}, dimensions={0} | all-to-all | bytes 5308416 | tf_op jit(solution)/shard_map/all_to_all | solution.py:26
  446.8 0.0 copy-done.2
  446.8 1.9 fusion
Async XLA Ops:
  7.2 111.4 %copy-start = (bf16[576,2304]{1,0:T(8,128)(2,1)S(1)}, bf16[576,2304]{1,0:T(8,128)(2,1)}, u32[]{:S(2)}) copy-start(bf16[576,2304]{1,0:T(8,128)(2,1)} %param.7) | copy-start | bytes 7962628
  7.2 111.4 %all-reduce.2.cloned.1.call-start = ((), (), s32[]{:S(2)}) async-start(), calls=%async_computation.3 | async-start | bytes 5898240 | tf_op jit(solution)/shard_map/psum | solution.py:44
  12.3 248.6 %reduce-scatter.2.cloned.1.call-start = ((), (), s32[]{:S(2)}) async-start(), calls=%async_computation.4 | async-start | bytes 10948608 | tf_op jit(solution)/shard_map/reduce_scatter | solution.py:45
  131.0 129.8 %copy-start.1 = (f32[72,2304]{1,0:T(8,128)S(1)}, f32[72,2304]{1,0:T(8,128)}, u32[]{:S(2)}) copy-start(f32[72,2304]{1,0:T(8,128)} %param.8) | copy-start | bytes 1990660
  131.1 211.4 %all-gather.2.cloned.1.call-start = ((), (), s32[]{:S(2)}) async-start(), calls=%async_computation.5 | async-start | bytes 10948608 | tf_op jit(solution)/shard_map/all_gather | solution.py:58
  406.3 40.5 %copy-start.2 = (bf16[288,2304]{1,0:T(8,128)(2,1)S(1)}, bf16[288,2304]{1,0:T(8,128)(2,1)}, u32[]{:S(2)}) copy-start(bf16[288,2304]{1,0:T(8,128)(2,1)} %param.6) | copy-start | bytes 3981316
Sparse Core Ops, SparseCore 0:
  12.4 106.1 all-reduce.1
  131.2 129.6 reduce-scatter.1
  263.6 78.8 all-gather.1
where the time goes:
time: 456 us; the launch traced here: 455 us
  waiting for transfers between devices  315 us (69%)
  blocking collectives  85.4 us (19%)
  matrix products  31.2 us (7%)
  between operations  13.8 us (3%)
  other arithmetic  4.99 us (1%)
  local copies, waits for them, and re-layouts  4.76 us (1%)
    reduce_scatter x1, waiting for transfers between devices, per_device(): lax.psum_scatter(jnp.dot(rotated_left, right_basis, preferred_element_typ...  130 us
    psum x1, waiting for transfers between devices, per_device(): rotated_left = lax.psum(partial_value.astype(jnp.bfloat16), 'row')  106 us
    all_gather x1, waiting for transfers between devices, per_device(): lax.all_gather(step_rot, 'col', axis=0, tiled=True)  79.1 us
    all_to_all x1, blocking collectives, sum_at_owner(): blocks = lax.all_to_all(cut_along(shard, dim, size), axis, 0, 0, tiled=True)  44.9 us
    all_to_all x1, blocking collectives, copy_for_each(): return lax.all_to_all(copies, axis, split_axis=0, concat_axis=0, tiled=True)  40.5 us
    dot_general x1, matrix products, per_device(): jnp.dot(rotated_left, right_basis, preferred_element_type=jnp.float32)  12.5 us
    dot_general x1, matrix products, per_device(): lax.dot_general(lax.all_gather(step_rot, 'col', axis=0, tiled=True), righ...  11.7 us
  transfers between devices with their start and end apart: 3, of which 3 were waited for; matrix products, arithmetic and copies ran while one was open for 0% of the time, Pallas kernels for 0%

commit v1 on v0

--- a/solution.py
+++ b/solution.py
@@ -41,7 +41,9 @@
     partial_value = lax.dot_general(
         left_basis, gradient, (((0,), (0,)), ((), ())), preferred_element_type=jnp.float32
     )
-    rotated_left = lax.psum(partial_value.astype(jnp.bfloat16), "row")
+    own = partial_value.astype(jnp.bfloat16)
+    parts = lax.all_gather(own, "row", axis=0, tiled=False)
+    rotated_left = parts.sum(axis=0)
     rotated = lax.psum_scatter(
         jnp.dot(rotated_left, right_basis, preferred_element_type=jnp.float32).astype(jnp.bfloat16),
         "col",

time: 456 us -> 643 us (1.41)
  waiting for transfers between devices: 315 us -> 442 us
  other arithmetic: 4.99 us -> 51.4 us
  local copies, waits for them, and re-layouts: 4.76 us -> 21.1 us
    all_gather x0 -> x1, waiting for transfers between devices: none -> 233 us  [per_device(): parts = lax.all_gather(own, 'row', axis=0, tiled=False)]
    psum x1 -> x0, waiting for transfers between devices: 106 us -> none  [per_device(): rotated_left = lax.psum(partial_value.astype(jnp.bfloat16), 'row')]
    reduce_sum x0 -> x1, other arithmetic: none -> 46.4 us  [per_device(): rotated_left = parts.sum(axis=0)]
    unnamed x6 -> x7, local copies, waits for them, and re-layouts: 0.02 us -> 16.3 us
where the time goes in v1:
time: 643 us
  waiting for transfers between devices  442 us (69%)
  blocking collectives  85.4 us (13%)
  other arithmetic  51.4 us (8%)
  matrix products  29.1 us (5%)
  local copies, waits for them, and re-layouts  21.1 us (3%)
  between operations  13.8 us (2%)
    all_gather x1, waiting for transfers between devices, per_device(): parts = lax.all_gather(own, 'row', axis=0, tiled=False)  233 us
    reduce_scatter x1, waiting for transfers between devices, per_device(): lax.psum_scatter(jnp.dot(rotated_left, right_basis, preferred_element_typ...  130 us
    all_gather x1, waiting for transfers between devices, per_device(): lax.all_gather(step_rot, 'col', axis=0, tiled=True)  77.9 us
    reduce_sum x1, other arithmetic, per_device(): rotated_left = parts.sum(axis=0)  46.4 us
    all_to_all x1, blocking collectives, sum_at_owner(): blocks = lax.all_to_all(cut_along(shard, dim, size), axis, 0, 0, tiled=True)  44.9 us
    all_to_all x1, blocking collectives, copy_for_each(): return lax.all_to_all(copies, axis, split_axis=0, concat_axis=0, tiled=True)  40.5 us
    unnamed x7, local copies, waits for them, and re-layouts  16.3 us
  transfers between devices with their start and end apart: 3, of which 3 were waited for; matrix products, arithmetic and copies ran while one was open for 0% of the time, Pallas kernels for 0%

profile of v1, /device:TPU:32, one launch (start us, length us, event | category | flops | bytes accessed | tf_op | source)
XLA Modules:
  0.0 642.7 jit_solution(6905320311075488674)
XLA Ops:
  7.2 0.0 copy-start
  7.2 0.0 all-gather.6.cloned.1.call-start
  7.2 4.6 convolution_convert_fusion.2
  11.9 0.0 all-gather.6.cloned.1.call-update
  11.9 0.0 reduce-scatter.2.cloned.1.call-start
  11.9 233.4 %all-gather.6.cloned.1.call-done = bf16[18432,576]{0,1:T(8,128)(2,1)} async-done(((bf16[2304,576]{0,1:T(8,128)(2,1)}), bf16[18432,576]{0,1:T(8,128)(2,1)}) %all-gather.6.cloned.1.call-update) | async-done | bytes 21233680 | tf_op jit(solution)/shard_map/all_gather | solution.py:45
  245.3 16.3 %copy.10 = bf16[72,8,8,2304]{3,2,1,0:T(8,128)(2,1)} copy(bf16[72,8,8,2304]{3,1,2,0:T(8,128)(2,1)} %bitcast.17) | data formatting | bytes 42467328
  261.6 46.4 %bitcast_reduce_fusion = bf16[2304,576]{0,1:T(8,128)(2,1)S(1)} fusion(bf16[72,8,8,2304]{3,2,1,0:T(8,128)(2,1)} %copy.10), kind=kLoop, calls=%fused_computation | loop fusion | flops 9289728 | bytes 23887872 | tf_op jit(solution)/shard_map/reduce_sum | solution.py:46
  308.1 0.0 copy-done
  308.1 10.8 %convolution_convert_fusion = bf16[2304,2304]{1,0:T(8,128)(2,1)} fusion(bf16[2304,576]{0,1:T(8,128)(2,1)S(1)} %bitcast_reduce_fusion, bf16[576,2304]{1,0:T(8,128)(2,1)S(1)} %copy-done), kind=kOutput, calls=%fused_computation.1 | convolution fusion | flops 6120603648 | bytes 15925248 | tf_op jit(solution)/shard_map/dot_general | solution.py:48
  318.9 0.0 copy-start.1
  318.9 0.0 reduce-scatter.2.cloned.1.call-update
  318.9 0.2 all-gather.4.cloned.1.call-start
  319.2 130.2 %reduce-scatter.2.cloned.1.call-done = bf16[72,2304]{1,0:T(8,128)(2,1)} async-done(((bf16[2304,2304]{1,0:T(8,128)(2,1)}), bf16[72,2304]{1,0:T(8,128)(2,1)}) %reduce-scatter.2.cloned.1.call-update) | async-done | bytes 331792 | tf_op jit(solution)/shard_map/reduce_scatter | solution.py:47
  449.4 0.0 copy-done.1
  449.4 2.6 divide_convert_fusion
  452.0 0.0 all-gather.4.cloned.1.call-update
  452.0 77.9 %all-gather.4.cloned.1.call-done = bf16[2304,2304]{1,0:T(8,128)(2,1)} async-done(((bf16[72,2304]{1,0:T(8,128)(2,1)}), bf16[2304,2304]{1,0:T(8,128)(2,1)}) %all-gather.4.cloned.1.call-update) | async-done | bytes 10616848 | tf_op jit(solution)/shard_map/all_gather | solution.py:60
  529.9 11.7 %convolution_convert_fusion.1 = bf16[2304,576]{0,1:T(8,128)(2,1)} fusion(bf16[2304,2304]{1,0:T(8,128)(2,1)} %all-gather.4.cloned.1.call-done, bf16[576,2304]{1,0:T(8,128)(2,1)S(1)} %copy-done), kind=kOutput, calls=%fused_computation.2 | convolution fusion | flops 6116622336 | bytes 15925248 | tf_op jit(solution)/shard_map/dot_general | solution.py:59
  541.6 4.5 copy.9
  546.1 44.9 %all_to_all.10 = bf16[8,288,576]{2,1,0:T(8,128)(2,1)} all-to-all(bf16[8,288,576]{2,1,0:T(8,128)(2,1)} %bitcast.18), channel_id=1, replica_groups=mesh['row'=8,'col'=32] {'row'}, dimensions={0} | all-to-all | bytes 5308416 | tf_op jit(solution)/shard_map/all_to_all | solution.py:20
  591.0 2.4 reduce_sum.25
  593.4 0.2 broadcast_in_dim.3
  593.7 0.0 copy-start.2
  593.7 40.5 %all_to_all.11 = bf16[8,288,576]{2,1,0:T(8,128)(2,1)S(1)} all-to-all(bf16[8,288,576]{2,1,0:T(8,128)(2,1)S(1)} %broadcast_in_dim.3), channel_id=1, replica_groups=mesh['row'=8,'col'=32] {'row'}, dimensions={0} | all-to-all | bytes 5308416 | tf_op jit(solution)/shard_map/all_to_all | solution.py:26
  634.2 0.0 copy-done.2
  634.2 1.9 fusion
Async XLA Ops:
  7.2 300.9 %copy-start = (bf16[576,2304]{1,0:T(8,128)(2,1)S(1)}, bf16[576,2304]{1,0:T(8,128)(2,1)}, u32[]{:S(2)}) copy-start(bf16[576,2304]{1,0:T(8,128)(2,1)} %param.7) | copy-start | bytes 7962628
  7.2 238.1 %all-gather.6.cloned.1.call-start = ((), (), s32[]{:S(2)}) async-start(), calls=%async_computation.5 | async-start | bytes 23887872 | tf_op jit(solution)/shard_map/all_gather | solution.py:45
  11.9 437.5 %reduce-scatter.2.cloned.1.call-start = ((), (), s32[]{:S(2)}) async-start(), calls=%async_computation.3 | async-start | bytes 10948608 | tf_op jit(solution)/shard_map/reduce_scatter | solution.py:47
  318.9 130.5 %copy-start.1 = (f32[72,2304]{1,0:T(8,128)S(1)}, f32[72,2304]{1,0:T(8,128)}, u32[]{:S(2)}) copy-start(f32[72,2304]{1,0:T(8,128)} %param.8) | copy-start | bytes 1990660
  318.9 211.0 %all-gather.4.cloned.1.call-start = ((), (), s32[]{:S(2)}) async-start(), calls=%async_computation.4 | async-start | bytes 10948608 | tf_op jit(solution)/shard_map/all_gather | solution.py:60
  593.7 40.5 %copy-start.2 = (bf16[288,2304]{1,0:T(8,128)(2,1)S(1)}, bf16[288,2304]{1,0:T(8,128)(2,1)}, u32[]{:S(2)}) copy-start(bf16[288,2304]{1,0:T(8,128)(2,1)} %param.6) | copy-start | bytes 3981316
Sparse Core Ops, SparseCore 0:
  12.0 233.2 all-gather.5
  319.1 130.2 reduce-scatter.1
  452.1 77.7 all-gather.3
